TPU v7x, 32 devices: a whole 2x2x4 slice. The times are simulated.
32 devices in a mesh: tok: 8 (over z, y), unit: 4 (over x, core).
Axes of the slice: x: 2, y: 2, z: 4, core: 2. Of those that a mesh axis runs over, the one named last changes fastest.
Arguments:
- act_a: bfloat16 [16384, 3072], P('tok', 'unit'), may hold values from -4000 to 4000
- act_b: bfloat16 [16384, 3072], P(('tok', 'unit')), may hold values from -4000 to 4000
Outputs:
- correlation: float32 [3072, 3072], P('tok', 'unit')
All inputs are finite; a program needn't handle non-finite values.
Results may differ from a plain program's by a relative error of at most 0.0003.
Values may be sent and summed in bfloat16 or wider, within the bound.
A program may use at most 128 MiB of HBM per device.

v0:
```python
import jax
import jax.numpy as jnp
from jax import lax
from jax.sharding import PartitionSpec as P


def contract_tokens(left, right):
    return lax.dot_general(
        left, right, (((0,), (0,)), ((), ())), preferred_element_type=jnp.float32
    )


def per_device(act_a, act_b):
    token_rows, own_units = act_a.shape
    units = act_b.shape[1]
    groups = lax.axis_size("tok")
    band = units // groups
    total_tokens = token_rows * groups
    wide_a = act_a.astype(jnp.float32)
    first_total = jnp.sum(wide_a, axis=0)
    first_square = jnp.sum(wide_a * wide_a, axis=0)
    piece = lax.all_gather(act_b, "unit", axis=0, tiled=True)
    product = contract_tokens(piece, act_a)
    wide_piece = piece.astype(jnp.float32)
    second_total = jnp.sum(wide_piece, axis=0)
    second_square = jnp.sum(wide_piece * wide_piece, axis=0)
    product, second_total, second_square = (product, second_total, second_square)
    shares = lax.psum_scatter(product, "tok", scatter_dimension=0, tiled=True)
    first_all, first_square_all, second_all, second_square_all = lax.psum(
        (first_total, first_square, second_total, second_square), "tok"
    )
    offset = lax.axis_index("tok") * band
    second_own = lax.dynamic_slice_in_dim(second_all, offset, band, 0)
    second_square_own = lax.dynamic_slice_in_dim(second_square_all, offset, band, 0)
    mean_a = first_all / total_tokens
    var_a = first_square_all / total_tokens - mean_a * mean_a
    mean_b = second_own / total_tokens
    var_b = second_square_own / total_tokens - mean_b * mean_b
    centered = shares / total_tokens - mean_b[:, None] * mean_a[None, :]
    return centered / (jnp.sqrt(var_b + 1e-05)[:, None] * jnp.sqrt(var_a + 1e-05)[None, :])


def solution(mesh):
    placed = (P("tok", "unit"), P(("tok", "unit"), None))
    return jax.shard_map(
        per_device, mesh=mesh, in_specs=placed, out_specs=P("tok", "unit"), check_vma=False
    )
```

profile of v0, /device:TPU:0, one launch (start us, length us, event | category | flops | bytes accessed | tf_op | source)
XLA Modules:
  0.0 281.4 jit_solution(8721838583599671117)
XLA Ops:
  6.5 0.0 copy-start
  6.5 0.0 all-gather.2.cloned.1.call-start
  6.5 0.7 all-gather.2.cloned.1.call-update
  7.3 0.0 reduce-scatter.2.cloned.1.call-start
  7.3 86.4 %all-gather.2.cloned.1.call-done = bf16[2048,3072]{1,0:T(8,128)(2,1)} async-done(((bf16[512,3072]{1,0:T(8,128)(2,1)}), bf16[2048,3072]{1,0:T(8,128)(2,1)}) %all-gather.2.cloned.1.call-update) | async-done | bytes 12582928 | tf_op jit(solution)/shard_map/all_gather | solution.py:22
  93.7 0.0 copy-done
  93.7 15.2 %fusion.2 = f32[3072,768]{1,0:T(8,128)} fusion(bf16[2048,3072]{1,0:T(8,128)(2,1)} %all-gather.2.cloned.1.call-done, bf16[2048,768]{1,0:T(8,128)(2,1)S(1)} %copy-done), kind=kOutput, calls=%fused_computation.11 | convolution fusion | flops 9663676416 | bytes 25165824 | tf_op jit(solution)/shard_map/dot_general | solution.py:8
  109.0 0.0 reduce-scatter.2.cloned.1.call-update
  109.0 0.9 convert_reduce_fusion.1
  109.9 8.0 %convert_reduce_fusion = (f32[3072]{0:T(1024)S(1)}, f32[3072]{0:T(1024)S(1)}) fusion(bf16[2048,3072]{1,0:T(8,128)(2,1)} %all-gather.2.cloned.1.call-done), kind=kLoop, calls=%fused_computation.1 | loop fusion | flops 25159680 | bytes 12607488 | tf_op jit(solution)/shard_map/reduce_sum | solution.py:25
  117.9 39.5 %all-reduce = (f32[768]{0:T(1024)S(1)}, f32[768]{0:T(1024)S(1)}, f32[3072]{0:T(1024)S(1)}, f32[3072]{0:T(1024)S(1)}) all-reduce(f32[768]{0:T(1024)S(1)} %get-tuple-element.8, f32[768]{0:T(1024)S(1)} %get-tuple-element.7, f32[3072]{0:T(1024)S(1)} %get-tuple-element.6, ...), channel_id=1, replica_groups=mesh['tok'=8,'unit'=4] {'tok'}, use_global_device_ids=true, to_apply=%region_8.0 | all-reduce | flops 7680 | bytes 61440 | tf_op jit(solution)/shard_map/psum | solution.py:29
  157.3 0.1 dynamic-slice_multiply_fusion
  157.4 114.6 %reduce-scatter.2.cloned.1.call-done = f32[384,768]{1,0:T(8,128)} async-done(((f32[3072,768]{1,0:T(8,128)}), f32[384,768]{1,0:T(8,128)}) %reduce-scatter.2.cloned.1.call-update) | async-done | bytes 1179664 | tf_op jit(solution)/shard_map/reduce_scatter | solution.py:28
  272.0 2.6 multiply_divide_fusion
  (1 shorter events, 0.0 us)
Async XLA Ops:
  6.5 87.2 %copy-start = (bf16[2048,768]{1,0:T(8,128)(2,1)S(1)}, bf16[2048,768]{1,0:T(8,128)(2,1)}, u32[]{:S(2)}) copy-start(bf16[2048,768]{1,0:T(8,128)(2,1)} %param.2) | copy-start | bytes 9437188
  6.5 87.2 %all-gather.2.cloned.1.call-start = ((), (), s32[]{:S(2)}) async-start(), calls=%async_computation.1 | async-start | bytes 15728640 | tf_op jit(solution)/shard_map/all_gather | solution.py:22
  7.3 264.7 %reduce-scatter.2.cloned.1.call-start = ((), (), s32[]{:S(2)}) async-start(), calls=%async_computation.2 | async-start | bytes 10616832 | tf_op jit(solution)/shard_map/reduce_scatter | solution.py:28
Sparse Core Ops, SparseCore 0:
  8.9 84.7 all-gather.1
  109.1 162.8 reduce-scatter.1
where the time goes:
time: 282 us; the launch traced here: 281 us
  waiting for transfers between devices  202 us (72%)
  blocking collectives  39.5 us (14%)
  matrix products  15.2 us (5%)
  between operations  13.4 us (5%)
  other arithmetic  11.5 us (4%)
    reduce_scatter x1, waiting for transfers between devices, per_device(): shares = lax.psum_scatter(product, 'tok', scatter_dimension=0, tiled=True)  115 us
    all_gather x1, waiting for transfers between devices, per_device(): piece = lax.all_gather(act_b, 'unit', axis=0, tiled=True)  86.4 us
    psum x1, blocking collectives, per_device(): lax.psum((first_total, first_square, second_total, second_square), 'tok')  39.5 us
    dot_general x1, matrix products, contract_tokens(): lax.dot_general(left, right, (((0,), (0,)), ((), ())), preferred_element_...  15.2 us
    reduce_sum x1, other arithmetic, per_device(): second_total = jnp.sum(wide_piece, axis=0)  8 us
  transfers between devices with their start and end apart: 2, of which 2 were waited for; matrix products, arithmetic and copies ran while one was open for 3% of the time, Pallas kernels for 0%

commit v1 on v0

--- a/solution.py
+++ b/solution.py
@@ -19,7 +19,16 @@
     wide_a = act_a.astype(jnp.float32)
     first_total = jnp.sum(wide_a, axis=0)
     first_square = jnp.sum(wide_a * wide_a, axis=0)
-    piece = lax.all_gather(act_b, "unit", axis=0, tiled=True)
+    handle_object = lambda s0, d_out: jnp.concatenate(
+        lax.all_to_all(
+            jnp.stack([s0 for _ in range(lax.axis_size("unit"))]),
+            "unit",
+            split_axis=0,
+            concat_axis=0,
+        ),
+        axis=d_out,
+    )
+    piece = handle_object(act_b, 0)
     product = contract_tokens(piece, act_a)
     wide_piece = piece.astype(jnp.float32)
     second_total = jnp.sum(wide_piece, axis=0)

time: 282 us -> 349 us (1.24)
  blocking collectives: 39.5 us -> 184 us
  waiting for transfers between devices: 202 us -> 115 us
  local copies, waits for them, and re-layouts: 0.01 us -> 12.6 us
    all_to_all x0 -> x1, blocking collectives: none -> 143 us  [per_device(): lax.all_to_all(jnp.stack([s0 for _ in range(lax.axis_size('unit'))]), 'un...]
    all_gather x1 -> x0, waiting for transfers between devices: 86.4 us -> none  [per_device(): piece = lax.all_gather(act_b, 'unit', axis=0, tiled=True)]
    another operation x0 -> x1, local copies, waits for them, and re-layouts: none -> 8.06 us  [per_device(): jnp.stack([s0 for _ in range(lax.axis_size('unit'))])]
    unnamed x2 -> x4, local copies, waits for them, and re-layouts: 0.01 us -> 4.57 us
  transfers between devices with their start and end apart: 2 -> 1, of which waited for: 2 -> 1; matrix products, arithmetic and copies ran while one was open for 3% -> 3% of each run, Pallas kernels for 0% -> 0%
where the time goes in v1:
time: 349 us
  blocking collectives  184 us (53%)
  waiting for transfers between devices  115 us (33%)
  between operations  13.4 us (4%)
  matrix products  12.9 us (4%)
  local copies, waits for them, and re-layouts  12.6 us (4%)
  other arithmetic  11.5 us (3%)
    all_to_all x1, blocking collectives, per_device(): lax.all_to_all(jnp.stack([s0 for _ in range(lax.axis_size('unit'))]), 'un...  143 us
    reduce_scatter x1, waiting for transfers between devices, per_device(): shares = lax.psum_scatter(product, 'tok', scatter_dimension=0, tiled=True)  115 us
    psum x1, blocking collectives, per_device(): lax.psum((first_total, first_square, second_total, second_square), 'tok')  40.6 us
    dot_general x1, matrix products, contract_tokens(): lax.dot_general(left, right, (((0,), (0,)), ((), ())), preferred_element_...  12.9 us
    another operation x1, local copies, waits for them, and re-layouts, per_device(): jnp.stack([s0 for _ in range(lax.axis_size('unit'))])  8.06 us
    reduce_sum x1, other arithmetic, per_device(): second_total = jnp.sum(wide_piece, axis=0)  8 us
  transfers between devices with their start and end apart: 1, of which 1 were waited for; matrix products, arithmetic and copies ran while one was open for 3% of the time, Pallas kernels for 0%

profile of v1, /device:TPU:0, one launch (start us, length us, event | category | flops | bytes accessed | tf_op | source)
XLA Modules:
  0.0 349.2 jit_solution(13224129377873912550)
XLA Ops:
  6.5 0.0 reduce-scatter.2.cloned.1.call-start
  6.5 8.1 %stack.2 = bf16[4,512,3072]{2,1,0:T(8,128)(2,1)} broadcast(bf16[512,3072]{1,0:T(8,128)(2,1)} %param.3), dimensions={1,2} | broadcast | bytes 15728640 | tf_op jit(solution)/shard_map/stack | solution.py:24
  14.6 0.0 copy-start.1
  14.6 143.4 %all_to_all.5 = bf16[4,512,3072]{2,1,0:T(8,128)(2,1)S(1)} all-to-all(bf16[4,512,3072]{2,1,0:T(8,128)(2,1)} %stack.2), channel_id=1, replica_groups=mesh['tok'=8,'unit'=4] {'unit'}, dimensions={0} | all-to-all | bytes 25165824 | tf_op jit(solution)/shard_map/all_to_all | solution.py:23
  158.0 0.0 copy-start
  158.0 4.6 %copy-done = bf16[4,512,3072]{2,1,0:T(8,128)(2,1)} copy-done((bf16[4,512,3072]{2,1,0:T(8,128)(2,1)}, bf16[4,512,3072]{2,1,0:T(8,128)(2,1)S(1)}, u32[]{:S(2)}) %copy-start) | copy-done | bytes 12582936
  162.6 0.0 copy-done.1
  162.6 12.9 %fusion.2 = f32[3072,768]{1,0:T(8,128)} fusion(bf16[2048,3072]{1,0:T(8,128)(2,1)S(1)} %bitcast.3, bf16[2048,768]{1,0:T(8,128)(2,1)S(1)} %copy-done.1), kind=kOutput, calls=%fused_computation.11 | convolution fusion | flops 9663676416 | bytes 25165824 | tf_op jit(solution)/shard_map/dot_general | solution.py:8
  175.5 0.0 reduce-scatter.2.cloned.1.call-update
  175.5 0.9 convert_reduce_fusion.1
  176.4 8.0 %convert_reduce_fusion = (f32[3072]{0:T(1024)S(1)}, f32[3072]{0:T(1024)S(1)}) fusion(bf16[4,512,3072]{2,1,0:T(8,128)(2,1)} %copy-done), kind=kLoop, calls=%fused_computation.1 | loop fusion | flops 25159680 | bytes 12607488 | tf_op jit(solution)/shard_map/reduce_sum | solution.py:34
  184.4 40.6 %all-reduce = (f32[768]{0:T(1024)S(1)}, f32[768]{0:T(1024)S(1)}, f32[3072]{0:T(1024)S(1)}, f32[3072]{0:T(1024)S(1)}) all-reduce(f32[768]{0:T(1024)S(1)} %get-tuple-element.8, f32[768]{0:T(1024)S(1)} %get-tuple-element.7, f32[3072]{0:T(1024)S(1)} %get-tuple-element.6, ...), channel_id=1, replica_groups=mesh['tok'=8,'unit'=4] {'tok'}, use_global_device_ids=true, to_apply=%region_8.0 | all-reduce | flops 7680 | bytes 61440 | tf_op jit(solution)/shard_map/psum | solution.py:38
  225.0 0.1 dynamic-slice_multiply_fusion
  225.1 114.7 %reduce-scatter.2.cloned.1.call-done = f32[384,768]{1,0:T(8,128)} async-done(((f32[3072,768]{1,0:T(8,128)}), f32[384,768]{1,0:T(8,128)}) %reduce-scatter.2.cloned.1.call-update) | async-done | bytes 1179664 | tf_op jit(solution)/shard_map/reduce_scatter | solution.py:37
  339.7 2.6 multiply_divide_fusion
  (1 shorter events, 0.0 us)
Async XLA Ops:
  6.5 333.2 %reduce-scatter.2.cloned.1.call-start = ((), (), s32[]{:S(2)}) async-start(), calls=%async_computation.2 | async-start | bytes 10616832 | tf_op jit(solution)/shard_map/reduce_scatter | solution.py:37
  14.6 148.0 %copy-start.1 = (bf16[2048,768]{1,0:T(8,128)(2,1)S(1)}, bf16[2048,768]{1,0:T(8,128)(2,1)}, u32[]{:S(2)}) copy-start(bf16[2048,768]{1,0:T(8,128)(2,1)} %param.2) | copy-start | bytes 9437188
  158.0 4.6 %copy-start = (bf16[4,512,3072]{2,1,0:T(8,128)(2,1)}, bf16[4,512,3072]{2,1,0:T(8,128)(2,1)S(1)}, u32[]{:S(2)}) copy-start(bf16[4,512,3072]{2,1,0:T(8,128)(2,1)S(1)} %all_to_all.5) | copy-start | bytes 37748740
Sparse Core Ops, SparseCore 0:
  175.6 164.0 reduce-scatter.1
